TPU v7x, 128 devices: a whole 4x4x4 slice. The times are simulated.
128 devices in a mesh: gx: 8 (over y, core), gy: 4 (over z), gz: 4 (over x).
Axes of the slice: x: 4, y: 4, z: 4, core: 2. Of those that a mesh axis runs over, the one named last changes fastest.
Arguments:
- kappa_sq: float32 [128, 64, 512], P('gx', 'gz', 'gy'), may hold values from 0.004 to 0.4
- probe_bits: int32 [4, 128, 64, 512], P(None, 'gx', 'gz', 'gy'), may hold values from 0 to 1
Outputs:
- solution: float32 [4, 128, 64, 512], P(None, 'gx', 'gz', 'gy')
- relative_residual: float32 [4], replicated
All inputs are finite; a program needn't handle non-finite values.
Results may differ from a plain program's by a relative error of at most 0.0001.
Values sent between devices are 32-bit elements; how exact they have to be, the bound alone decides.
A program may use at most 128 MiB of HBM per device.

v0:
```python
import jax
import jax.numpy as jnp
from jax import lax
from jax.sharding import Mesh
from jax.sharding import PartitionSpec as P

LEVELS = 3
COARSE_SWEEPS = 8
ITERS = 2
GX_GY_GZ = ("gx_0", "gx_1", "gy", "gz")
GX = ("gx_0", "gx_1")
damping = 0.8


def extended(block, sides, width):
    for axis, dim in sides:
        count = lax.axis_size(axis)
        forward = [(i, i + 1) for i in range(count - 1)]
        backward = [(target, source) for source, target in forward]
        low = lax.ppermute(
            lax.slice_in_dim(block, block.shape[dim] - width, None, axis=dim), axis, forward
        )
        high = lax.ppermute(lax.slice_in_dim(block, 0, width, axis=dim), axis, backward)
        block = jnp.concatenate([low, block, high], axis=dim)
    return block


def extended_2(value, sides, width):
    edges = {}
    for axis, dim in sides:
        size, length = (lax.axis_size(axis), value.shape[dim])
        up = [(i, (i + 1) % size) for i in range(size - 1)]
        last = lax.slice_in_dim(value, length - width, length, axis=dim)
        first = lax.slice_in_dim(value, 0, width, axis=dim)
        edges[dim] = (
            lax.ppermute(last, axis, up),
            lax.ppermute(first, axis, [(b, a) for a, b in up]),
        )
    done = []
    for _, dim in sides:
        low, high = edges[dim]
        around = [(width, width) if d in done else (0, 0) for d in range(value.ndim)]
        value = jnp.concatenate([jnp.pad(low, around), value, jnp.pad(high, around)], axis=dim)
        done.append(dim)
    return value


def over_axes(value, axes):
    for axis in axes:
        value = lax.psum(value, axis)
    return value


def neighbours(padded):
    along_first = padded[..., 2:, 1:-1, 1:-1] + padded[..., :-2, 1:-1, 1:-1]
    along_second = padded[..., 1:-1, 2:, 1:-1] + padded[..., 1:-1, :-2, 1:-1]
    along_third = padded[..., 1:-1, 1:-1, 2:] + padded[..., 1:-1, 1:-1, :-2]
    return along_first + along_second + along_third


def coarsen(field):
    leading = field.shape[:-3]
    cells_first, cells_second, cells_third = field.shape[-3:]
    grouped = field.reshape(
        leading + (cells_first // 2, 2, cells_second // 2, 2, cells_third // 2, 2)
    )
    return jnp.mean(grouped, axis=(-5, -3, -1))


def refine(field):
    leading = field.shape[:-3]
    cells_first, cells_second, cells_third = field.shape[-3:]
    spread = field.reshape(leading + (cells_first, 1, cells_second, 1, cells_third, 1))
    spread = jnp.broadcast_to(spread, leading + (cells_first, 2, cells_second, 2, cells_third, 2))
    return spread.reshape(leading + (cells_first * 2, cells_second * 2, cells_third * 2))


def level_faces(field, grid_level):
    if grid_level == 0:
        return extended(field, ((GX, 1), ("gy", 3), ("gz", 2)), 1)
    return extended_2(field, ((GX, 1), ("gy", 3), ("gz", 2)), 1)


def operate(field, diagonal, coupling, grid_level):
    return diagonal * field - coupling * neighbours(level_faces(field, grid_level))


def jacobi_sweep(field, rhs_field, diagonal, coupling, grid_level):
    return field + damping * (rhs_field - operate(field, diagonal, coupling, grid_level)) / diagonal


def assemble(gathered):
    count_x = lax.axis_size(GX)
    count_y = lax.axis_size("gy")
    count_z = lax.axis_size("gz")
    leading = gathered.shape[1:-3]
    cells_first, cells_second, cells_third = gathered.shape[-3:]
    lead_count = len(leading)
    blocks = gathered.reshape(
        (count_x, count_y, count_z) + leading + (cells_first, cells_second, cells_third)
    )
    permutation = tuple(range(3, 3 + lead_count)) + (
        0,
        3 + lead_count,
        2,
        4 + lead_count,
        1,
        5 + lead_count,
    )
    blocks = jnp.transpose(blocks, permutation)
    return blocks.reshape(
        leading + (count_x * cells_first, count_z * cells_second, count_y * cells_third)
    )


def local_dot(first_field, second_field):
    return jnp.sum(first_field * second_field, axis=(1, 2, 3))


def expand(values):
    return values[:, None, None, None]


def per_device(kappa_sq, probe_bits):
    diagonals = []
    couplings = []
    coef_field = kappa_sq
    for grid_level in range(LEVELS + 1):
        if grid_level > 0:
            coef_field = coarsen(coef_field)
        coupling = 0.25**grid_level
        diagonals.append(coef_field + 6.0 * coupling)
        couplings.append(coupling)
    global_diag = assemble(lax.all_gather(diagonals[LEVELS][None], GX_GY_GZ, axis=0, tiled=True))

    def coarsest(rhs_field):
        diagonal = diagonals[LEVELS]
        coupling = couplings[LEVELS]
        global_rhs = assemble(lax.all_gather(rhs_field[None], GX_GY_GZ, axis=0, tiled=True))
        field = damping * global_rhs / global_diag
        for sweep_index in range(COARSE_SWEEPS - 1):
            padded = jnp.pad(field, ((0, 0), (1, 1), (1, 1), (1, 1)))
            field = (
                field
                + damping
                * (global_rhs - (global_diag * field - coupling * neighbours(padded)))
                / global_diag
            )
        probes, block_x, block_z, block_y = rhs_field.shape
        zero_index = jnp.zeros((), jnp.int32)
        starts = (
            zero_index,
            lax.axis_index(GX) * block_x,
            lax.axis_index("gz") * block_z,
            lax.axis_index("gy") * block_y,
        )
        return lax.dynamic_slice(field, starts, (probes, block_x, block_z, block_y))

    def vcycle(rhs_field, grid_level):
        if grid_level == LEVELS:
            return coarsest(rhs_field)
        diagonal = diagonals[grid_level]
        coupling = couplings[grid_level]
        field = damping * rhs_field / diagonal
        field = jacobi_sweep(field, rhs_field, diagonal, coupling, grid_level)
        remainder = rhs_field - operate(field, diagonal, coupling, grid_level)
        field = field + refine(vcycle(coarsen(remainder), grid_level + 1))
        field = jacobi_sweep(field, rhs_field, diagonal, coupling, grid_level)
        return jacobi_sweep(field, rhs_field, diagonal, coupling, grid_level)

    right_side = 2.0 * probe_bits.astype(jnp.float32) - 1.0
    solution = jnp.zeros_like(right_side)
    residual = right_side
    fine_diag = diagonals[0]

    def pair_sums(residual_now, precond_now, operated_now):
        return (
            over_axes(local_dot(residual_now, precond_now), GX_GY_GZ),
            over_axes(local_dot(precond_now, operated_now), GX_GY_GZ),
        )

    precond = vcycle(residual, 0)
    operated = operate(precond, fine_diag, 1.0, 0)
    precond_dot, curve_dot = pair_sums(residual, precond, operated)
    step_size = precond_dot / curve_dot
    search = precond
    along = operated
    for iteration in range(ITERS):
        solution = solution + expand(step_size) * search
        residual = residual - expand(step_size) * along
        if iteration + 1 < ITERS:
            precond = vcycle(residual, 0)
            operated = operate(precond, fine_diag, 1.0, 0)
            next_dot, curve_dot = pair_sums(residual, precond, operated)
            ratio_next = next_dot / precond_dot
            step_size = next_dot / (curve_dot - ratio_next * next_dot / step_size)
            search = precond + expand(ratio_next) * search
            along = operated + expand(ratio_next) * along
            precond_dot = next_dot
    squares = lax.psum(local_dot(residual, residual), GX_GY_GZ)
    cell_total = (
        probe_bits.shape[1]
        * probe_bits.shape[2]
        * probe_bits.shape[3]
        * lax.axis_size(GX)
        * lax.axis_size("gy")
        * lax.axis_size("gz")
    )
    return (solution, jnp.sqrt(squares / cell_total))


def solution(mesh):
    finer = Mesh(
        mesh.devices.reshape(4, 2, mesh.shape["gy"], mesh.shape["gz"]), ("gx_0", "gx_1", "gy", "gz")
    )
    placed = (P(GX, "gz", "gy"), P(None, GX, "gz", "gy"))
    return jax.shard_map(
        per_device,
        mesh=finer,
        in_specs=placed,
        out_specs=(P(None, GX, "gz", "gy"), P()),
        check_vma=False,
    )
```

profile of v0, /device:TPU:1, one launch (start us, length us, event | category | flops | bytes accessed | tf_op | source)
XLA Modules:
  0.0 1092.7 jit_solution(3623767073840948052)
XLA Ops:
  2.7 4.6 collective-permute-start.1
  37.2 9.7 reshape.124
  72.7 8.8 copy.2403
  81.5 13.1 %reduce_sum.126 = f32[4,8,8,64]{0,3,2,1:T(8,128)} reduce(f32[4,8,2,8,2,64,2]{0,6,5,4,3,2,1:T(2,128)} %bitcast.21, f32[]{:T(128)} %constant.28.clone.1), dimensions={2,4,6}, to_apply=%region_0.0 | reduce | flops 114688 | bytes 589828 | tf_op jit(solution)/shard_map/reduce_sum | solution.py:67
  98.4 5.2 collective-permute-start.13
  118.1 5.1 collective-permute-start.19
  131.7 62.1 %all-gather.1 = f32[256,2,16]{2,1,0:T(2,128)S(1)} all-gather(f32[2,2,16]{2,1,0:T(2,128)S(1)} %multiply_add_fusion.2), channel_id=3, replica_groups=mesh['gx_0'=4,'gx_1'=2,'gy'=4,'gz'=4] {'gx_0','gx_1','gy','gz'}, dimensions={0}, use_global_device_ids=true | all-gather | bytes 33024 | tf_op jit(solution)/shard_map/all_gather | solution.py:134
  223.0 5.0 collective-permute-start.31
  244.9 61.7 %all-gather = f32[512,2,2,16]{3,2,1,0:T(2,128)S(1)} all-gather(f32[4,2,2,16]{3,2,1,0:T(2,128)S(1)} %copy.2408), channel_id=2, replica_groups=mesh['gx_0'=4,'gx_1'=2,'gy'=4,'gz'=4] {'gx_0','gx_1','gy','gz'}, dimensions={0}, use_global_device_ids=true | all-gather | bytes 132096 | tf_op jit(solution)/shard_map/all_gather | solution.py:139
  327.3 5.7 collective-permute-start.43
  354.4 6.2 collective-permute-start.49
  369.4 5.0 collective-permute-done.51
  380.1 6.2 collective-permute-start.55
  394.9 5.1 collective-permute-done.57
  407.8 9.0 broadcast_in_dim.14
  416.8 10.0 copy.2416
  426.9 6.2 collective-permute-start.61
  440.8 4.7 collective-permute-start.62
  495.7 4.5 collective-permute-start.74
  510.5 7.5 all-reduce.83
  518.0 6.0 all-reduce.85
  524.0 10.6 all-reduce.81
  534.6 6.0 all-reduce.79
  540.8 5.5 collective-permute-start.79
  585.9 4.7 collective-permute-start.86
  601.5 8.8 copy.2467
  610.3 13.1 %reduce_sum.134 = f32[4,8,8,64]{0,3,2,1:T(8,128)} reduce(f32[4,8,2,8,2,64,2]{0,6,5,4,3,2,1:T(2,128)} %bitcast.23, f32[]{:T(128)} %constant.28.clone.1), dimensions={2,4,6}, to_apply=%region_16.17 | reduce | flops 114688 | bytes 589828 | tf_op jit(solution)/shard_map/reduce_sum | solution.py:67
  638.8 5.2 collective-permute-done.93
  651.2 4.6 collective-permute-start.97
  664.5 5.1 collective-permute-done.99
  681.1 5.6 collective-permute-start.103
  703.5 6.2 collective-permute-start.109
  726.6 60.6 %all-gather.2 = f32[512,2,2,16]{3,2,1,0:T(2,128)S(1)} all-gather(f32[4,2,2,16]{3,2,1,0:T(2,128)S(1)} %copy.2472), channel_id=4, replica_groups=mesh['gx_0'=4,'gx_1'=2,'gy'=4,'gz'=4] {'gx_0','gx_1','gy','gz'}, dimensions={0}, use_global_device_ids=true | all-gather | bytes 132096 | tf_op jit(solution)/shard_map/all_gather | solution.py:139
  810.3 5.7 collective-permute-start.121
  837.4 6.2 collective-permute-start.127
  852.3 5.0 collective-permute-done.129
  862.9 6.2 collective-permute-start.133
  877.8 5.1 collective-permute-done.135
  890.6 9.0 broadcast_in_dim.17
  899.6 10.0 copy.2478
  909.7 6.2 collective-permute-start.139
  923.7 4.7 collective-permute-start.140
  966.3 4.5 collective-permute-start.151
  994.2 7.5 all-reduce.82
  1001.7 6.0 all-reduce.84
  1007.7 10.6 all-reduce.80
  1018.3 6.0 all-reduce.78
  1026.5 65.5 %psum.135 = f32[4]{0:T(128)S(1)} all-reduce(f32[4]{0:T(128)S(1)} %get-tuple-element.200), channel_id=1, replica_groups=mesh['gx_0'=4,'gx_1'=2,'gy'=4,'gz'=4] {'gx_0','gx_1','gy','gz'}, use_global_device_ids=true, to_apply=%region_30.31 | all-reduce | flops 4 | bytes 32 | tf_op jit(solution)/shard_map/psum | solution.py:200
  (606 shorter events, 542.9 us)
Async XLA Ops:
  31.1 20.0 %collective-permute-start.7 = (f32[4,1,16,128]{3,2,1,0:T(8,128)S(1)}, f32[4,1,16,128]{3,2,1,0:T(8,128)S(1)}, u32[]{:S(2)}, u32[]{:S(2)}) collective-permute-start(f32[4,1,16,128]{3,2,1,0:T(8,128)S(1)} %get-tuple-element.96), channel_id=1, source_target_pairs={{0,16},{16,32},{32,48},{48,64},{64,80},{80,96},{96,112},{1,17},{17... | collective-permute-start | bytes 98312 | tf_op jit(solution)/shard_map/ppermute | solution.py:20
  35.3 15.8 %collective-permute-start.6 = (f32[4,1,16,128]{3,2,1,0:T(8,128)S(1)}, f32[4,1,16,128]{3,2,1,0:T(8,128)S(1)}, u32[]{:S(2)}, u32[]{:S(2)}) collective-permute-start(f32[4,1,16,128]{3,2,1,0:T(8,128)S(1)} %get-tuple-element.97), channel_id=1, source_target_pairs={{16,0},{32,16},{48,32},{64,48},{80,64},{96,80},{112,96},{17,1},{33... | collective-permute-start | bytes 98312 | tf_op jit(solution)/shard_map/ppermute | solution.py:23
  98.4 19.2 %collective-permute-start.13 = (f32[4,1,8,64]{3,2,1,0:T(8,128)S(1)}, f32[4,1,8,64]{3,2,1,0:T(8,128)S(1)}, u32[]{:S(2)}, u32[]{:S(2)}) collective-permute-start(f32[4,1,8,64]{3,2,1,0:T(8,128)S(1)} %get-tuple-element.194), channel_id=1, source_target_pairs={{0,16},{16,32},{32,48},{48,64},{64,80},{80,96},{96,112},{1,17},{17... | collective-permute-start | bytes 24584 | tf_op jit(solution)/shard_map/ppermute | solution.py:36
  118.1 79.0 %collective-permute-start.19 = (f32[4,1,8,64]{3,2,1,0:T(8,128)S(1)}, f32[4,1,8,64]{3,2,1,0:T(8,128)S(1)}, u32[]{:S(2)}, u32[]{:S(2)}) collective-permute-start(f32[4,1,8,64]{3,2,1,0:T(8,128)S(1)} %get-tuple-element.188), channel_id=1, source_target_pairs={{0,16},{16,32},{32,48},{48,64},{64,80},{80,96},{96,112},{1,17},{17... | collective-permute-start | bytes 24584 | tf_op jit(solution)/shard_map/ppermute | solution.py:36
  123.1 73.9 %collective-permute-start.18 = (f32[4,1,8,64]{3,2,1,0:T(8,128)S(1)}, f32[4,1,8,64]{3,2,1,0:T(8,128)S(1)}, u32[]{:S(2)}, u32[]{:S(2)}) collective-permute-start(f32[4,1,8,64]{3,2,1,0:T(8,128)S(1)} %get-tuple-element.189), channel_id=1, source_target_pairs={{16,0},{32,16},{48,32},{64,48},{80,64},{96,80},{112,96},{17,1},{33... | collective-permute-start | bytes 24584 | tf_op jit(solution)/shard_map/ppermute | solution.py:37
  125.1 72.0 %collective-permute-start.22 = (f32[4,8,1,64]{3,2,1,0:T(1,128)S(1)}, f32[4,8,1,64]{3,2,1,0:T(1,128)S(1)}, u32[]{:S(2)}, u32[]{:S(2)}) collective-permute-start(f32[4,8,1,64]{3,2,1,0:T(1,128)S(1)} %get-tuple-element.184), channel_id=1, source_target_pairs={{1,0},{2,1},{3,2},{5,4},{6,5},{7,6},{9,8},{10,9},{11,10},{13,12},{... | collective-permute-start | bytes 24584 | tf_op jit(solution)/shard_map/ppermute | solution.py:37
  126.4 70.7 %collective-permute-start.23 = (f32[4,8,1,64]{3,2,1,0:T(1,128)S(1)}, f32[4,8,1,64]{3,2,1,0:T(1,128)S(1)}, u32[]{:S(2)}, u32[]{:S(2)}) collective-permute-start(f32[4,8,1,64]{3,2,1,0:T(1,128)S(1)} %get-tuple-element.185), channel_id=1, source_target_pairs={{0,1},{1,2},{2,3},{4,5},{5,6},{6,7},{8,9},{9,10},{10,11},{12,13},{... | collective-permute-start | bytes 24584 | tf_op jit(solution)/shard_map/ppermute | solution.py:36
  130.4 63.4 %collective-permute-start.21 = (f32[4,8,8,1]{3,2,1,0:T(8,128)S(1)}, f32[4,8,8,1]{3,2,1,0:T(8,128)S(1)}, u32[]{:S(2)}, u32[]{:S(2)}) collective-permute-start(f32[4,8,8,1]{3,2,1,0:T(8,128)S(1)} %get-tuple-element.186), channel_id=1, source_target_pairs={{4,0},{8,4},{12,8},{5,1},{9,5},{13,9},{6,2},{10,6},{14,10},{7,3},{... | collective-permute-start | bytes 3080 | tf_op jit(solution)/shard_map/ppermute | solution.py:37
  202.6 20.1 %collective-permute-start.25 = (f32[4,1,4,32]{0,3,2,1:T(8,128)S(1)}, f32[4,1,4,32]{0,3,2,1:T(8,128)S(1)}, u32[]{:S(2)}, u32[]{:S(2)}) collective-permute-start(f32[4,1,4,32]{0,3,2,1:T(8,128)S(1)} %get-tuple-element.146), channel_id=1, source_target_pairs={{0,16},{16,32},{32,48},{48,64},{64,80},{80,96},{96,112},{1,17},{17... | collective-permute-start | bytes 6152 | tf_op jit(solution)/shard_map/ppermute | solution.py:36
  205.0 17.8 %collective-permute-start.24 = (f32[4,1,4,32]{0,3,2,1:T(8,128)S(1)}, f32[4,1,4,32]{0,3,2,1:T(8,128)S(1)}, u32[]{:S(2)}, u32[]{:S(2)}) collective-permute-start(f32[4,1,4,32]{0,3,2,1:T(8,128)S(1)} %get-tuple-element.147), channel_id=1, source_target_pairs={{16,0},{32,16},{48,32},{64,48},{80,64},{96,80},{112,96},{17,1},{33... | collective-permute-start | bytes 6152 | tf_op jit(solution)/shard_map/ppermute | solution.py:37
  223.0 21.3 %collective-permute-start.31 = (f32[4,1,4,32]{0,3,2,1:T(8,128)S(1)}, f32[4,1,4,32]{0,3,2,1:T(8,128)S(1)}, u32[]{:S(2)}, u32[]{:S(2)}) collective-permute-start(f32[4,1,4,32]{0,3,2,1:T(8,128)S(1)} %get-tuple-element.140), channel_id=1, source_target_pairs={{0,16},{16,32},{32,48},{48,64},{64,80},{80,96},{96,112},{1,17},{17... | collective-permute-start | bytes 6152 | tf_op jit(solution)/shard_map/ppermute | solution.py:36
  228.0 16.4 %collective-permute-start.30 = (f32[4,1,4,32]{0,3,2,1:T(8,128)S(1)}, f32[4,1,4,32]{0,3,2,1:T(8,128)S(1)}, u32[]{:S(2)}, u32[]{:S(2)}) collective-permute-start(f32[4,1,4,32]{0,3,2,1:T(8,128)S(1)} %get-tuple-element.141), channel_id=1, source_target_pairs={{16,0},{32,16},{48,32},{64,48},{80,64},{96,80},{112,96},{17,1},{33... | collective-permute-start | bytes 6152 | tf_op jit(solution)/shard_map/ppermute | solution.py:37
  309.5 17.5 %collective-permute-start.37 = (f32[4,1,4,32]{0,3,2,1:T(8,128)S(1)}, f32[4,1,4,32]{0,3,2,1:T(8,128)S(1)}, u32[]{:S(2)}, u32[]{:S(2)}) collective-permute-start(f32[4,1,4,32]{0,3,2,1:T(8,128)S(1)} %get-tuple-element.134), channel_id=1, source_target_pairs={{0,16},{16,32},{32,48},{48,64},{64,80},{80,96},{96,112},{1,17},{17... | collective-permute-start | bytes 6152 | tf_op jit(solution)/shard_map/ppermute | solution.py:36
  311.4 15.6 %collective-permute-start.36 = (f32[4,1,4,32]{0,3,2,1:T(8,128)S(1)}, f32[4,1,4,32]{0,3,2,1:T(8,128)S(1)}, u32[]{:S(2)}, u32[]{:S(2)}) collective-permute-start(f32[4,1,4,32]{0,3,2,1:T(8,128)S(1)} %get-tuple-element.135), channel_id=1, source_target_pairs={{16,0},{32,16},{48,32},{64,48},{80,64},{96,80},{112,96},{17,1},{33... | collective-permute-start | bytes 6152 | tf_op jit(solution)/shard_map/ppermute | solution.py:37
  327.3 22.1 %collective-permute-start.43 = (f32[4,1,4,32]{0,3,2,1:T(8,128)S(1)}, f32[4,1,4,32]{0,3,2,1:T(8,128)S(1)}, u32[]{:S(2)}, u32[]{:S(2)}) collective-permute-start(f32[4,1,4,32]{0,3,2,1:T(8,128)S(1)} %get-tuple-element.128), channel_id=1, source_target_pairs={{0,16},{16,32},{32,48},{48,64},{64,80},{80,96},{96,112},{1,17},{17... | collective-permute-start | bytes 6152 | tf_op jit(solution)/shard_map/ppermute | solution.py:36
  333.0 16.4 %collective-permute-start.42 = (f32[4,1,4,32]{0,3,2,1:T(8,128)S(1)}, f32[4,1,4,32]{0,3,2,1:T(8,128)S(1)}, u32[]{:S(2)}, u32[]{:S(2)}) collective-permute-start(f32[4,1,4,32]{0,3,2,1:T(8,128)S(1)} %get-tuple-element.129), channel_id=1, source_target_pairs={{16,0},{32,16},{48,32},{64,48},{80,64},{96,80},{112,96},{17,1},{33... | collective-permute-start | bytes 6152 | tf_op jit(solution)/shard_map/ppermute | solution.py:37
  354.4 25.3 %collective-permute-start.49 = (f32[4,1,8,64]{3,2,1,0:T(8,128)S(1)}, f32[4,1,8,64]{3,2,1,0:T(8,128)S(1)}, u32[]{:S(2)}, u32[]{:S(2)}) collective-permute-start(f32[4,1,8,64]{3,2,1,0:T(8,128)S(1)} %get-tuple-element.182), channel_id=1, source_target_pairs={{0,16},{16,32},{32,48},{48,64},{64,80},{80,96},{96,112},{1,17},{17... | collective-permute-start | bytes 24584 | tf_op jit(solution)/shard_map/ppermute | solution.py:36
  360.6 19.1 %collective-permute-start.48 = (f32[4,1,8,64]{3,2,1,0:T(8,128)S(1)}, f32[4,1,8,64]{3,2,1,0:T(8,128)S(1)}, u32[]{:S(2)}, u32[]{:S(2)}) collective-permute-start(f32[4,1,8,64]{3,2,1,0:T(8,128)S(1)} %get-tuple-element.183), channel_id=1, source_target_pairs={{16,0},{32,16},{48,32},{64,48},{80,64},{96,80},{112,96},{17,1},{33... | collective-permute-start | bytes 24584 | tf_op jit(solution)/shard_map/ppermute | solution.py:37
  362.6 17.2 %collective-permute-start.52 = (f32[4,8,1,64]{3,2,1,0:T(1,128)S(1)}, f32[4,8,1,64]{3,2,1,0:T(1,128)S(1)}, u32[]{:S(2)}, u32[]{:S(2)}) collective-permute-start(f32[4,8,1,64]{3,2,1,0:T(1,128)S(1)} %get-tuple-element.178), channel_id=1, source_target_pairs={{1,0},{2,1},{3,2},{5,4},{6,5},{7,6},{9,8},{10,9},{11,10},{13,12},{... | collective-permute-start | bytes 24584 | tf_op jit(solution)/shard_map/ppermute | solution.py:37
  364.0 15.7 %collective-permute-start.53 = (f32[4,8,1,64]{3,2,1,0:T(1,128)S(1)}, f32[4,8,1,64]{3,2,1,0:T(1,128)S(1)}, u32[]{:S(2)}, u32[]{:S(2)}) collective-permute-start(f32[4,8,1,64]{3,2,1,0:T(1,128)S(1)} %get-tuple-element.179), channel_id=1, source_target_pairs={{0,1},{1,2},{2,3},{4,5},{5,6},{6,7},{8,9},{9,10},{10,11},{12,13},{... | collective-permute-start | bytes 24584 | tf_op jit(solution)/shard_map/ppermute | solution.py:36
  380.1 25.3 %collective-permute-start.55 = (f32[4,1,8,64]{3,2,1,0:T(8,128)S(1)}, f32[4,1,8,64]{3,2,1,0:T(8,128)S(1)}, u32[]{:S(2)}, u32[]{:S(2)}) collective-permute-start(f32[4,1,8,64]{3,2,1,0:T(8,128)S(1)} %get-tuple-element.176), channel_id=1, source_target_pairs={{0,16},{16,32},{32,48},{48,64},{64,80},{80,96},{96,112},{1,17},{17... | collective-permute-start | bytes 24584 | tf_op jit(solution)/shard_map/ppermute | solution.py:36
  386.3 19.1 %collective-permute-start.54 = (f32[4,1,8,64]{3,2,1,0:T(8,128)S(1)}, f32[4,1,8,64]{3,2,1,0:T(8,128)S(1)}, u32[]{:S(2)}, u32[]{:S(2)}) collective-permute-start(f32[4,1,8,64]{3,2,1,0:T(8,128)S(1)} %get-tuple-element.177), channel_id=1, source_target_pairs={{16,0},{32,16},{48,32},{64,48},{80,64},{96,80},{112,96},{17,1},{33... | collective-permute-start | bytes 24584 | tf_op jit(solution)/shard_map/ppermute | solution.py:37
  388.2 17.1 %collective-permute-start.58 = (f32[4,8,1,64]{3,2,1,0:T(1,128)S(1)}, f32[4,8,1,64]{3,2,1,0:T(1,128)S(1)}, u32[]{:S(2)}, u32[]{:S(2)}) collective-permute-start(f32[4,8,1,64]{3,2,1,0:T(1,128)S(1)} %get-tuple-element.172), channel_id=1, source_target_pairs={{1,0},{2,1},{3,2},{5,4},{6,5},{7,6},{9,8},{10,9},{11,10},{13,12},{... | collective-permute-start | bytes 24584 | tf_op jit(solution)/shard_map/ppermute | solution.py:37
  389.5 15.9 %collective-permute-start.59 = (f32[4,8,1,64]{3,2,1,0:T(1,128)S(1)}, f32[4,8,1,64]{3,2,1,0:T(1,128)S(1)}, u32[]{:S(2)}, u32[]{:S(2)}) collective-permute-start(f32[4,8,1,64]{3,2,1,0:T(1,128)S(1)} %get-tuple-element.173), channel_id=1, source_target_pairs={{0,1},{1,2},{2,3},{4,5},{5,6},{6,7},{8,9},{9,10},{10,11},{12,13},{... | collective-permute-start | bytes 24584 | tf_op jit(solution)/shard_map/ppermute | solution.py:36
  625.7 25.1 %collective-permute-start.91 = (f32[4,1,8,64]{3,2,1,0:T(8,128)S(1)}, f32[4,1,8,64]{3,2,1,0:T(8,128)S(1)}, u32[]{:S(2)}, u32[]{:S(2)}) collective-permute-start(f32[4,1,8,64]{3,2,1,0:T(8,128)S(1)} %get-tuple-element.170), channel_id=1, source_target_pairs={{0,16},{16,32},{32,48},{48,64},{64,80},{80,96},{96,112},{1,17},{17... | collective-permute-start | bytes 24584 | tf_op jit(solution)/shard_map/ppermute | solution.py:36
  629.8 21.1 %collective-permute-start.90 = (f32[4,1,8,64]{3,2,1,0:T(8,128)S(1)}, f32[4,1,8,64]{3,2,1,0:T(8,128)S(1)}, u32[]{:S(2)}, u32[]{:S(2)}) collective-permute-start(f32[4,1,8,64]{3,2,1,0:T(8,128)S(1)} %get-tuple-element.171), channel_id=1, source_target_pairs={{16,0},{32,16},{48,32},{64,48},{80,64},{96,80},{112,96},{17,1},{33... | collective-permute-start | bytes 24584 | tf_op jit(solution)/shard_map/ppermute | solution.py:37
  631.7 19.1 %collective-permute-start.94 = (f32[4,8,1,64]{3,2,1,0:T(1,128)S(1)}, f32[4,8,1,64]{3,2,1,0:T(1,128)S(1)}, u32[]{:S(2)}, u32[]{:S(2)}) collective-permute-start(f32[4,8,1,64]{3,2,1,0:T(1,128)S(1)} %get-tuple-element.166), channel_id=1, source_target_pairs={{1,0},{2,1},{3,2},{5,4},{6,5},{7,6},{9,8},{10,9},{11,10},{13,12},{... | collective-permute-start | bytes 24584 | tf_op jit(solution)/shard_map/ppermute | solution.py:37
  633.0 17.8 %collective-permute-start.95 = (f32[4,8,1,64]{3,2,1,0:T(1,128)S(1)}, f32[4,8,1,64]{3,2,1,0:T(1,128)S(1)}, u32[]{:S(2)}, u32[]{:S(2)}) collective-permute-start(f32[4,8,1,64]{3,2,1,0:T(1,128)S(1)} %get-tuple-element.167), channel_id=1, source_target_pairs={{0,1},{1,2},{2,3},{4,5},{5,6},{6,7},{8,9},{9,10},{10,11},{12,13},{... | collective-permute-start | bytes 24584 | tf_op jit(solution)/shard_map/ppermute | solution.py:36
  651.2 24.3 %collective-permute-start.97 = (f32[4,1,8,64]{3,2,1,0:T(8,128)S(1)}, f32[4,1,8,64]{3,2,1,0:T(8,128)S(1)}, u32[]{:S(2)}, u32[]{:S(2)}) collective-permute-start(f32[4,1,8,64]{3,2,1,0:T(8,128)S(1)} %get-tuple-element.164), channel_id=1, source_target_pairs={{0,16},{16,32},{32,48},{48,64},{64,80},{80,96},{96,112},{1,17},{17... | collective-permute-start | bytes 24584 | tf_op jit(solution)/shard_map/ppermute | solution.py:36
  655.9 19.6 %collective-permute-start.96 = (f32[4,1,8,64]{3,2,1,0:T(8,128)S(1)}, f32[4,1,8,64]{3,2,1,0:T(8,128)S(1)}, u32[]{:S(2)}, u32[]{:S(2)}) collective-permute-start(f32[4,1,8,64]{3,2,1,0:T(8,128)S(1)} %get-tuple-element.165), channel_id=1, source_target_pairs={{16,0},{32,16},{48,32},{64,48},{80,64},{96,80},{112,96},{17,1},{33... | collective-permute-start | bytes 24584 | tf_op jit(solution)/shard_map/ppermute | solution.py:37
  657.8 17.7 %collective-permute-start.100 = (f32[4,8,1,64]{3,2,1,0:T(1,128)S(1)}, f32[4,8,1,64]{3,2,1,0:T(1,128)S(1)}, u32[]{:S(2)}, u32[]{:S(2)}) collective-permute-start(f32[4,8,1,64]{3,2,1,0:T(1,128)S(1)} %get-tuple-element.160), channel_id=1, source_target_pairs={{1,0},{2,1},{3,2},{5,4},{6,5},{7,6},{9,8},{10,9},{11,10},{13,12},{... | collective-permute-start | bytes 24584 | tf_op jit(solution)/shard_map/ppermute | solution.py:37
  659.1 16.4 %collective-permute-start.101 = (f32[4,8,1,64]{3,2,1,0:T(1,128)S(1)}, f32[4,8,1,64]{3,2,1,0:T(1,128)S(1)}, u32[]{:S(2)}, u32[]{:S(2)}) collective-permute-start(f32[4,8,1,64]{3,2,1,0:T(1,128)S(1)} %get-tuple-element.161), channel_id=1, source_target_pairs={{0,1},{1,2},{2,3},{4,5},{5,6},{6,7},{8,9},{9,10},{10,11},{12,13},{... | collective-permute-start | bytes 24584 | tf_op jit(solution)/shard_map/ppermute | solution.py:36
  681.1 22.1 %collective-permute-start.103 = (f32[4,1,4,32]{0,3,2,1:T(8,128)S(1)}, f32[4,1,4,32]{0,3,2,1:T(8,128)S(1)}, u32[]{:S(2)}, u32[]{:S(2)}) collective-permute-start(f32[4,1,4,32]{0,3,2,1:T(8,128)S(1)} %get-tuple-element.122), channel_id=1, source_target_pairs={{0,16},{16,32},{32,48},{48,64},{64,80},{80,96},{96,112},{1,17},{17... | collective-permute-start | bytes 6152 | tf_op jit(solution)/shard_map/ppermute | solution.py:36
  686.7 16.5 %collective-permute-start.102 = (f32[4,1,4,32]{0,3,2,1:T(8,128)S(1)}, f32[4,1,4,32]{0,3,2,1:T(8,128)S(1)}, u32[]{:S(2)}, u32[]{:S(2)}) collective-permute-start(f32[4,1,4,32]{0,3,2,1:T(8,128)S(1)} %get-tuple-element.123), channel_id=1, source_target_pairs={{16,0},{32,16},{48,32},{64,48},{80,64},{96,80},{112,96},{17,1},{33... | collective-permute-start | bytes 6152 | tf_op jit(solution)/shard_map/ppermute | solution.py:37
  703.5 22.6 %collective-permute-start.109 = (f32[4,1,4,32]{0,3,2,1:T(8,128)S(1)}, f32[4,1,4,32]{0,3,2,1:T(8,128)S(1)}, u32[]{:S(2)}, u32[]{:S(2)}) collective-permute-start(f32[4,1,4,32]{0,3,2,1:T(8,128)S(1)} %get-tuple-element.116), channel_id=1, source_target_pairs={{0,16},{16,32},{32,48},{48,64},{64,80},{80,96},{96,112},{1,17},{17... | collective-permute-start | bytes 6152 | tf_op jit(solution)/shard_map/ppermute | solution.py:36
  709.7 16.4 %collective-permute-start.108 = (f32[4,1,4,32]{0,3,2,1:T(8,128)S(1)}, f32[4,1,4,32]{0,3,2,1:T(8,128)S(1)}, u32[]{:S(2)}, u32[]{:S(2)}) collective-permute-start(f32[4,1,4,32]{0,3,2,1:T(8,128)S(1)} %get-tuple-element.117), channel_id=1, source_target_pairs={{16,0},{32,16},{48,32},{64,48},{80,64},{96,80},{112,96},{17,1},{33... | collective-permute-start | bytes 6152 | tf_op jit(solution)/shard_map/ppermute | solution.py:37
  792.3 17.7 %collective-permute-start.115 = (f32[4,1,4,32]{0,3,2,1:T(8,128)S(1)}, f32[4,1,4,32]{0,3,2,1:T(8,128)S(1)}, u32[]{:S(2)}, u32[]{:S(2)}) collective-permute-start(f32[4,1,4,32]{0,3,2,1:T(8,128)S(1)} %get-tuple-element.110), channel_id=1, source_target_pairs={{0,16},{16,32},{32,48},{48,64},{64,80},{80,96},{96,112},{1,17},{17... | collective-permute-start | bytes 6152 | tf_op jit(solution)/shard_map/ppermute | solution.py:36
  794.2 15.8 %collective-permute-start.114 = (f32[4,1,4,32]{0,3,2,1:T(8,128)S(1)}, f32[4,1,4,32]{0,3,2,1:T(8,128)S(1)}, u32[]{:S(2)}, u32[]{:S(2)}) collective-permute-start(f32[4,1,4,32]{0,3,2,1:T(8,128)S(1)} %get-tuple-element.111), channel_id=1, source_target_pairs={{16,0},{32,16},{48,32},{64,48},{80,64},{96,80},{112,96},{17,1},{33... | collective-permute-start | bytes 6152 | tf_op jit(solution)/shard_map/ppermute | solution.py:37
  810.3 22.1 %collective-permute-start.121 = (f32[4,1,4,32]{0,3,2,1:T(8,128)S(1)}, f32[4,1,4,32]{0,3,2,1:T(8,128)S(1)}, u32[]{:S(2)}, u32[]{:S(2)}) collective-permute-start(f32[4,1,4,32]{0,3,2,1:T(8,128)S(1)} %get-tuple-element.104), channel_id=1, source_target_pairs={{0,16},{16,32},{32,48},{48,64},{64,80},{80,96},{96,112},{1,17},{17... | collective-permute-start | bytes 6152 | tf_op jit(solution)/shard_map/ppermute | solution.py:36
  816.1 16.4 %collective-permute-start.120 = (f32[4,1,4,32]{0,3,2,1:T(8,128)S(1)}, f32[4,1,4,32]{0,3,2,1:T(8,128)S(1)}, u32[]{:S(2)}, u32[]{:S(2)}) collective-permute-start(f32[4,1,4,32]{0,3,2,1:T(8,128)S(1)} %get-tuple-element.105), channel_id=1, source_target_pairs={{16,0},{32,16},{48,32},{64,48},{80,64},{96,80},{112,96},{17,1},{33... | collective-permute-start | bytes 6152 | tf_op jit(solution)/shard_map/ppermute | solution.py:37
  837.4 25.1 %collective-permute-start.127 = (f32[4,1,8,64]{3,2,1,0:T(8,128)S(1)}, f32[4,1,8,64]{3,2,1,0:T(8,128)S(1)}, u32[]{:S(2)}, u32[]{:S(2)}) collective-permute-start(f32[4,1,8,64]{3,2,1,0:T(8,128)S(1)} %get-tuple-element.158), channel_id=1, source_target_pairs={{0,16},{16,32},{32,48},{48,64},{64,80},{80,96},{96,112},{1,17},{17... | collective-permute-start | bytes 24584 | tf_op jit(solution)/shard_map/ppermute | solution.py:36
  843.7 18.9 %collective-permute-start.126 = (f32[4,1,8,64]{3,2,1,0:T(8,128)S(1)}, f32[4,1,8,64]{3,2,1,0:T(8,128)S(1)}, u32[]{:S(2)}, u32[]{:S(2)}) collective-permute-start(f32[4,1,8,64]{3,2,1,0:T(8,128)S(1)} %get-tuple-element.159), channel_id=1, source_target_pairs={{16,0},{32,16},{48,32},{64,48},{80,64},{96,80},{112,96},{17,1},{33... | collective-permute-start | bytes 24584 | tf_op jit(solution)/shard_map/ppermute | solution.py:37
  845.6 17.0 %collective-permute-start.130 = (f32[4,8,1,64]{3,2,1,0:T(1,128)S(1)}, f32[4,8,1,64]{3,2,1,0:T(1,128)S(1)}, u32[]{:S(2)}, u32[]{:S(2)}) collective-permute-start(f32[4,8,1,64]{3,2,1,0:T(1,128)S(1)} %get-tuple-element.154), channel_id=1, source_target_pairs={{1,0},{2,1},{3,2},{5,4},{6,5},{7,6},{9,8},{10,9},{11,10},{13,12},{... | collective-permute-start | bytes 24584 | tf_op jit(solution)/shard_map/ppermute | solution.py:37
  846.9 15.7 %collective-permute-start.131 = (f32[4,8,1,64]{3,2,1,0:T(1,128)S(1)}, f32[4,8,1,64]{3,2,1,0:T(1,128)S(1)}, u32[]{:S(2)}, u32[]{:S(2)}) collective-permute-start(f32[4,8,1,64]{3,2,1,0:T(1,128)S(1)} %get-tuple-element.155), channel_id=1, source_target_pairs={{0,1},{1,2},{2,3},{4,5},{5,6},{6,7},{8,9},{9,10},{10,11},{12,13},{... | collective-permute-start | bytes 24584 | tf_op jit(solution)/shard_map/ppermute | solution.py:36
  862.9 25.3 %collective-permute-start.133 = (f32[4,1,8,64]{3,2,1,0:T(8,128)S(1)}, f32[4,1,8,64]{3,2,1,0:T(8,128)S(1)}, u32[]{:S(2)}, u32[]{:S(2)}) collective-permute-start(f32[4,1,8,64]{3,2,1,0:T(8,128)S(1)} %get-tuple-element.152), channel_id=1, source_target_pairs={{0,16},{16,32},{32,48},{48,64},{64,80},{80,96},{96,112},{1,17},{17... | collective-permute-start | bytes 24584 | tf_op jit(solution)/shard_map/ppermute | solution.py:36
  869.2 19.1 %collective-permute-start.132 = (f32[4,1,8,64]{3,2,1,0:T(8,128)S(1)}, f32[4,1,8,64]{3,2,1,0:T(8,128)S(1)}, u32[]{:S(2)}, u32[]{:S(2)}) collective-permute-start(f32[4,1,8,64]{3,2,1,0:T(8,128)S(1)} %get-tuple-element.153), channel_id=1, source_target_pairs={{16,0},{32,16},{48,32},{64,48},{80,64},{96,80},{112,96},{17,1},{33... | collective-permute-start | bytes 24584 | tf_op jit(solution)/shard_map/ppermute | solution.py:37
  871.1 17.1 %collective-permute-start.136 = (f32[4,8,1,64]{3,2,1,0:T(1,128)S(1)}, f32[4,8,1,64]{3,2,1,0:T(1,128)S(1)}, u32[]{:S(2)}, u32[]{:S(2)}) collective-permute-start(f32[4,8,1,64]{3,2,1,0:T(1,128)S(1)} %get-tuple-element.148), channel_id=1, source_target_pairs={{1,0},{2,1},{3,2},{5,4},{6,5},{7,6},{9,8},{10,9},{11,10},{13,12},{... | collective-permute-start | bytes 24584 | tf_op jit(solution)/shard_map/ppermute | solution.py:37
  872.4 15.9 %collective-permute-start.137 = (f32[4,8,1,64]{3,2,1,0:T(1,128)S(1)}, f32[4,8,1,64]{3,2,1,0:T(1,128)S(1)}, u32[]{:S(2)}, u32[]{:S(2)}) collective-permute-start(f32[4,8,1,64]{3,2,1,0:T(1,128)S(1)} %get-tuple-element.149), channel_id=1, source_target_pairs={{0,1},{1,2},{2,3},{4,5},{5,6},{6,7},{8,9},{9,10},{10,11},{12,13},{... | collective-permute-start | bytes 24584 | tf_op jit(solution)/shard_map/ppermute | solution.py:36
  (118 other events, 976.2 us)
where the time goes:
time: 1110 us; the launch traced here: 1090 us
  starting transfers between devices  431 us (39%)
  blocking collectives  310 us (28%)
  waiting for transfers between devices  159 us (14%)
  local copies, waits for them, and re-layouts  122 us (11%)
  other arithmetic  67.4 us (6%)
    ppermute x48, starting transfers between devices, extended_2(): lax.ppermute(last, axis, up)  195 us
    all_gather x2, blocking collectives, coarsest(): lax.all_gather(rhs_field[None], GX_GY_GZ, axis=0, tiled=True)  122 us
    ppermute x30, starting transfers between devices, extended(): lax.ppermute(lax.slice_in_dim(block, block.shape[dim] - width, None, axis...  116 us
    ppermute x48, starting transfers between devices, extended_2(): lax.ppermute(first, axis, [(b, a) for a, b in up])  74.5 us
    ppermute x30, waiting for transfers between devices, extended(): lax.ppermute(lax.slice_in_dim(block, 0, width, axis=dim), axis, backward)  71.7 us
    psum x1, blocking collectives, per_device(): squares = lax.psum(local_dot(residual, residual), GX_GY_GZ)  65.5 us
    all_gather x1, blocking collectives, per_device(): lax.all_gather(diagonals[LEVELS][None], GX_GY_GZ, axis=0, tiled=True)  62.1 us
    psum x8, blocking collectives, over_axes(): value = lax.psum(value, axis)  60.2 us
  transfers between devices with their start and end apart: 156, of which 68 were waited for; matrix products, arithmetic and copies ran while one was open for 2% of the time, Pallas kernels for 0%

commit v1 on v0

--- a/solution.py
+++ b/solution.py
@@ -136,7 +136,14 @@
     def coarsest(rhs_field):
         diagonal = diagonals[LEVELS]
         coupling = couplings[LEVELS]
-        global_rhs = assemble(lax.all_gather(rhs_field[None], GX_GY_GZ, axis=0, tiled=True))
+        global_rhs = assemble(
+            jnp.concatenate(
+                lax.all_to_all(
+                    jnp.stack([rhs_field[None]] * lax.axis_size(GX_GY_GZ)), GX_GY_GZ, 0, 0
+                ),
+                axis=0,
+            )
+        )
         field = damping * global_rhs / global_diag
         for sweep_index in range(COARSE_SWEEPS - 1):
             padded = jnp.pad(field, ((0, 0), (1, 1), (1, 1), (1, 1)))

time: 1110 us -> 1040 us (0.937)
  blocking collectives: 310 us -> 208 us
  starting transfers between devices: 431 us -> 445 us
  local copies, waits for them, and re-layouts: 122 us -> 134 us
    all_gather x2 -> x0, blocking collectives: 122 us -> none  [coarsest(): lax.all_gather(rhs_field[None], GX_GY_GZ, axis=0, tiled=True)]
    all_to_all x0 -> x1, blocking collectives: none -> 21 us  [coarsest(): lax.all_to_all(jnp.stack([rhs_field[None]] * lax.axis_size(GX_GY_GZ)), GX...]
    all_to_all x0 -> x1, starting transfers between devices: none -> 11.4 us  [coarsest(): lax.all_to_all(jnp.stack([rhs_field[None]] * lax.axis_size(GX_GY_GZ)), GX...]
  transfers between devices with their start and end apart: 156 -> 157, of which waited for: 68 -> 69; matrix products, arithmetic and copies ran while one was open for 2% -> 3% of each run, Pallas kernels for 0% -> 0%
where the time goes in v1:
time: 1040 us; the launch traced here: 1020 us
  starting transfers between devices  445 us (43%)
  blocking collectives  208 us (20%)
  waiting for transfers between devices  162 us (16%)
  local copies, waits for them, and re-layouts  134 us (13%)
  other arithmetic  69.2 us (7%)
    ppermute x48, starting transfers between devices, extended_2(): lax.ppermute(last, axis, up)  200 us
    ppermute x30, starting transfers between devices, extended(): lax.ppermute(lax.slice_in_dim(block, block.shape[dim] - width, None, axis...  116 us
    ppermute x48, starting transfers between devices, extended_2(): lax.ppermute(first, axis, [(b, a) for a, b in up])  72.7 us
    ppermute x30, waiting for transfers between devices, extended(): lax.ppermute(lax.slice_in_dim(block, 0, width, axis=dim), axis, backward)  72 us
    psum x1, blocking collectives, per_device(): squares = lax.psum(local_dot(residual, residual), GX_GY_GZ)  65.5 us
    ppermute x48, waiting for transfers between devices, extended_2(): lax.ppermute(first, axis, [(b, a) for a, b in up])  63.7 us
    all_gather x1, blocking collectives, per_device(): lax.all_gather(diagonals[LEVELS][None], GX_GY_GZ, axis=0, tiled=True)  62 us
    psum x8, blocking collectives, over_axes(): value = lax.psum(value, axis)  59.2 us
  transfers between devices with their start and end apart: 157, of which 69 were waited for; matrix products, arithmetic and copies ran while one was open for 3% of the time, Pallas kernels for 0%

profile of v1, /device:TPU:1, one launch (start us, length us, event | category | flops | bytes accessed | tf_op | source)
XLA Modules:
  0.0 1022.6 jit_solution(9989817607021942956)
XLA Ops:
  2.7 4.6 collective-permute-start.1
  47.2 9.7 reshape.112
  71.9 8.7 copy.2403
  80.6 13.1 %reduce_sum.126 = f32[4,8,8,64]{0,3,2,1:T(8,128)} reduce(f32[4,8,2,8,2,64,2]{0,6,5,4,3,2,1:T(2,128)} %bitcast.21, f32[]{:T(128)} %constant.28.clone.1), dimensions={2,4,6}, to_apply=%region_0.0 | reduce | flops 114688 | bytes 589828 | tf_op jit(solution)/shard_map/reduce_sum | solution.py:67
  108.9 4.8 collective-permute-done.15
  121.7 5.3 collective-permute-start.19
  134.3 4.7 collective-permute-start.20
  146.5 5.1 collective-permute-start.25
  168.6 5.9 collective-permute-start.31
  194.1 11.4 %all-to-all-start = ((f32[128,1,256]{2,1,0:T(1,128)}), f32[128,1,256]{2,1,0:T(1,128)S(1)}, u32[]{:S(2)}, u32[]{:S(2)}) async-start(f32[128,1,256]{2,1,0:T(1,128)} %reshape.129), calls=%async_computation | async-start | bytes 262144 | tf_op jit(solution)/shard_map/all_to_all | solution.py:141
  205.6 62.0 %all-gather = f32[256,2,16]{2,1,0:T(2,128)S(1)} all-gather(f32[2,2,16]{2,1,0:T(2,128)S(1)} %multiply_add_fusion.2), channel_id=2, replica_groups=mesh['gx_0'=4,'gx_1'=2,'gy'=4,'gz'=4] {'gx_0','gx_1','gy','gz'}, dimensions={0}, use_global_device_ids=true | all-gather | bytes 33024 | tf_op jit(solution)/shard_map/all_gather | solution.py:134
  290.7 5.4 collective-permute-start.43
  317.5 6.2 collective-permute-start.49
  332.4 5.0 collective-permute-done.51
  343.0 6.2 collective-permute-start.55
  357.9 5.1 collective-permute-done.57
  370.7 8.9 broadcast_in_dim.14
  379.6 10.0 copy.2416
  389.7 6.2 collective-permute-start.61
  403.7 4.9 collective-permute-start.62
  473.4 7.5 all-reduce.83
  480.9 6.0 all-reduce.85
  486.9 10.6 %all-reduce.81 = (f32[4]{0:T(128)S(1)}, f32[4]{0:T(128)S(1)}) all-reduce(f32[4]{0:T(128)S(1)} %get-tuple-element.32, f32[4]{0:T(128)S(1)} %get-tuple-element.33), channel_id=1, replica_groups=mesh['gx_0'=4,'gx_1'=2,'gy'=4,'gz'=4] {'gy'}, use_global_device_ids=true, to_apply=%region_9.10 | all-reduce | flops 8 | bytes 64 | tf_op jit(solution)/shard_map/psum | solution.py:50
  497.5 6.0 all-reduce.79
  503.7 5.5 collective-permute-start.79
  548.8 4.7 collective-permute-start.86
  564.3 8.7 copy.2467
  573.1 13.1 %reduce_sum.134 = f32[4,8,8,64]{0,3,2,1:T(8,128)} reduce(f32[4,8,2,8,2,64,2]{0,6,5,4,3,2,1:T(2,128)} %bitcast.23, f32[]{:T(128)} %constant.28.clone.1), dimensions={2,4,6}, to_apply=%region_16.17 | reduce | flops 114688 | bytes 589828 | tf_op jit(solution)/shard_map/reduce_sum | solution.py:67
  601.2 5.2 collective-permute-done.93
  613.6 4.6 collective-permute-start.97
  626.9 5.1 collective-permute-done.99
  643.5 5.6 collective-permute-start.103
  665.9 6.2 collective-permute-start.109
  693.1 21.0 %all_to_all.10 = f32[128,1,256]{2,1,0:T(1,128)S(1)} all-to-all(f32[128,1,256]{2,1,0:T(1,128)S(1)} %reshape.131), channel_id=1, replica_groups=mesh['gx_0'=4,'gx_1'=2,'gy'=4,'gz'=4] {'gx_0','gx_1','gy','gz'}, dimensions={0} | all-to-all | bytes 262144 | tf_op jit(solution)/shard_map/all_to_all | solution.py:141
  741.8 6.2 collective-permute-start.121
  769.4 6.2 collective-permute-start.127
  784.2 5.0 collective-permute-done.129
  794.9 6.2 collective-permute-start.133
  809.7 5.1 collective-permute-done.135
  822.6 8.9 broadcast_in_dim.17
  831.5 10.0 copy.2478
  841.6 6.2 collective-permute-start.139
  855.6 4.7 collective-permute-start.140
  924.8 6.2 all-reduce.82
  931.0 6.3 all-reduce.84
  937.4 10.6 %all-reduce.80 = (f32[4]{0:T(128)S(1)}, f32[4]{0:T(128)S(1)}) all-reduce(f32[4]{0:T(128)S(1)} %get-tuple-element.30, f32[4]{0:T(128)S(1)} %get-tuple-element.31), channel_id=1, replica_groups=mesh['gx_0'=4,'gx_1'=2,'gy'=4,'gz'=4] {'gy'}, use_global_device_ids=true, to_apply=%region_22.23 | all-reduce | flops 8 | bytes 64 | tf_op jit(solution)/shard_map/psum | solution.py:50
  948.0 6.0 all-reduce.78
  956.1 65.5 %psum.135 = f32[4]{0:T(128)S(1)} all-reduce(f32[4]{0:T(128)S(1)} %get-tuple-element.200), channel_id=1, replica_groups=mesh['gx_0'=4,'gx_1'=2,'gy'=4,'gz'=4] {'gx_0','gx_1','gy','gz'}, use_global_device_ids=true, to_apply=%region_30.31 | all-reduce | flops 4 | bytes 32 | tf_op jit(solution)/shard_map/psum | solution.py:207
  (616 shorter events, 561.7 us)
Async XLA Ops:
  41.2 19.9 %collective-permute-start.9 = (f32[4,18,16,1]{1,2,3,0:T(8,128)S(1)}, f32[4,18,16,1]{1,2,3,0:T(8,128)S(1)}, u32[]{:S(2)}, u32[]{:S(2)}) collective-permute-start(f32[4,18,16,1]{1,2,3,0:T(8,128)S(1)} %copy.2394), channel_id=1, source_target_pairs={{4,0},{8,4},{12,8},{5,1},{9,5},{13,9},{6,2},{10,6},{14,10},{7,3},{... | collective-permute-start | bytes 13832 | tf_op jit(solution)/shard_map/ppermute | solution.py:23
  42.9 18.6 %collective-permute-start.8 = (f32[4,18,16,1]{1,2,3,0:T(8,128)S(1)}, f32[4,18,16,1]{1,2,3,0:T(8,128)S(1)}, u32[]{:S(2)}, u32[]{:S(2)}) collective-permute-start(f32[4,18,16,1]{1,2,3,0:T(8,128)S(1)} %copy.2393), channel_id=1, source_target_pairs={{0,4},{4,8},{8,12},{1,5},{5,9},{9,13},{2,6},{6,10},{10,14},{3,7},{... | collective-permute-start | bytes 13832 | tf_op jit(solution)/shard_map/ppermute | solution.py:20
  96.1 23.9 %collective-permute-start.13 = (f32[4,1,8,64]{3,2,1,0:T(8,128)S(1)}, f32[4,1,8,64]{3,2,1,0:T(8,128)S(1)}, u32[]{:S(2)}, u32[]{:S(2)}) collective-permute-start(f32[4,1,8,64]{3,2,1,0:T(8,128)S(1)} %get-tuple-element.194), channel_id=1, source_target_pairs={{0,16},{16,32},{32,48},{48,64},{64,80},{80,96},{96,112},{1,17},{17... | collective-permute-start | bytes 24584 | tf_op jit(solution)/shard_map/ppermute | solution.py:36
  100.3 19.6 %collective-permute-start.12 = (f32[4,1,8,64]{3,2,1,0:T(8,128)S(1)}, f32[4,1,8,64]{3,2,1,0:T(8,128)S(1)}, u32[]{:S(2)}, u32[]{:S(2)}) collective-permute-start(f32[4,1,8,64]{3,2,1,0:T(8,128)S(1)} %get-tuple-element.195), channel_id=1, source_target_pairs={{16,0},{32,16},{48,32},{64,48},{80,64},{96,80},{112,96},{17,1},{33... | collective-permute-start | bytes 24584 | tf_op jit(solution)/shard_map/ppermute | solution.py:37
  102.3 17.7 %collective-permute-start.16 = (f32[4,8,1,64]{3,2,1,0:T(1,128)S(1)}, f32[4,8,1,64]{3,2,1,0:T(1,128)S(1)}, u32[]{:S(2)}, u32[]{:S(2)}) collective-permute-start(f32[4,8,1,64]{3,2,1,0:T(1,128)S(1)} %get-tuple-element.190), channel_id=1, source_target_pairs={{1,0},{2,1},{3,2},{5,4},{6,5},{7,6},{9,8},{10,9},{11,10},{13,12},{... | collective-permute-start | bytes 24584 | tf_op jit(solution)/shard_map/ppermute | solution.py:37
  103.6 16.4 %collective-permute-start.17 = (f32[4,8,1,64]{3,2,1,0:T(1,128)S(1)}, f32[4,8,1,64]{3,2,1,0:T(1,128)S(1)}, u32[]{:S(2)}, u32[]{:S(2)}) collective-permute-start(f32[4,8,1,64]{3,2,1,0:T(1,128)S(1)} %get-tuple-element.191), channel_id=1, source_target_pairs={{0,1},{1,2},{2,3},{4,5},{5,6},{6,7},{8,9},{9,10},{10,11},{12,13},{... | collective-permute-start | bytes 24584 | tf_op jit(solution)/shard_map/ppermute | solution.py:36
  121.7 19.2 %collective-permute-start.19 = (f32[4,1,8,64]{3,2,1,0:T(8,128)S(1)}, f32[4,1,8,64]{3,2,1,0:T(8,128)S(1)}, u32[]{:S(2)}, u32[]{:S(2)}) collective-permute-start(f32[4,1,8,64]{3,2,1,0:T(8,128)S(1)} %get-tuple-element.188), channel_id=1, source_target_pairs={{0,16},{16,32},{32,48},{48,64},{64,80},{80,96},{96,112},{1,17},{17... | collective-permute-start | bytes 24584 | tf_op jit(solution)/shard_map/ppermute | solution.py:36
  146.5 21.8 %collective-permute-start.25 = (f32[4,1,4,32]{0,3,2,1:T(8,128)S(1)}, f32[4,1,4,32]{0,3,2,1:T(8,128)S(1)}, u32[]{:S(2)}, u32[]{:S(2)}) collective-permute-start(f32[4,1,4,32]{0,3,2,1:T(8,128)S(1)} %get-tuple-element.146), channel_id=1, source_target_pairs={{0,16},{16,32},{32,48},{48,64},{64,80},{80,96},{96,112},{1,17},{17... | collective-permute-start | bytes 6152 | tf_op jit(solution)/shard_map/ppermute | solution.py:36
  151.5 16.8 %collective-permute-start.24 = (f32[4,1,4,32]{0,3,2,1:T(8,128)S(1)}, f32[4,1,4,32]{0,3,2,1:T(8,128)S(1)}, u32[]{:S(2)}, u32[]{:S(2)}) collective-permute-start(f32[4,1,4,32]{0,3,2,1:T(8,128)S(1)} %get-tuple-element.147), channel_id=1, source_target_pairs={{16,0},{32,16},{48,32},{64,48},{80,64},{96,80},{112,96},{17,1},{33... | collective-permute-start | bytes 6152 | tf_op jit(solution)/shard_map/ppermute | solution.py:37
  153.5 14.9 %collective-permute-start.28 = (f32[4,4,1,32]{0,3,2,1:T(8,128)S(1)}, f32[4,4,1,32]{0,3,2,1:T(8,128)S(1)}, u32[]{:S(2)}, u32[]{:S(2)}) collective-permute-start(f32[4,4,1,32]{0,3,2,1:T(8,128)S(1)} %get-tuple-element.142), channel_id=1, source_target_pairs={{1,0},{2,1},{3,2},{5,4},{6,5},{7,6},{9,8},{10,9},{11,10},{13,12},{... | collective-permute-start | bytes 6152 | tf_op jit(solution)/shard_map/ppermute | solution.py:37
  168.6 22.6 %collective-permute-start.31 = (f32[4,1,4,32]{0,3,2,1:T(8,128)S(1)}, f32[4,1,4,32]{0,3,2,1:T(8,128)S(1)}, u32[]{:S(2)}, u32[]{:S(2)}) collective-permute-start(f32[4,1,4,32]{0,3,2,1:T(8,128)S(1)} %get-tuple-element.140), channel_id=1, source_target_pairs={{0,16},{16,32},{32,48},{48,64},{64,80},{80,96},{96,112},{1,17},{17... | collective-permute-start | bytes 6152 | tf_op jit(solution)/shard_map/ppermute | solution.py:36
  174.6 16.6 %collective-permute-start.30 = (f32[4,1,4,32]{0,3,2,1:T(8,128)S(1)}, f32[4,1,4,32]{0,3,2,1:T(8,128)S(1)}, u32[]{:S(2)}, u32[]{:S(2)}) collective-permute-start(f32[4,1,4,32]{0,3,2,1:T(8,128)S(1)} %get-tuple-element.141), channel_id=1, source_target_pairs={{16,0},{32,16},{48,32},{64,48},{80,64},{96,80},{112,96},{17,1},{33... | collective-permute-start | bytes 6152 | tf_op jit(solution)/shard_map/ppermute | solution.py:37
  194.1 73.8 %all-to-all-start = ((f32[128,1,256]{2,1,0:T(1,128)}), f32[128,1,256]{2,1,0:T(1,128)S(1)}, u32[]{:S(2)}, u32[]{:S(2)}) async-start(f32[128,1,256]{2,1,0:T(1,128)} %reshape.129), calls=%async_computation | async-start | bytes 262144 | tf_op jit(solution)/shard_map/all_to_all | solution.py:141
  273.9 16.5 %collective-permute-start.37 = (f32[4,1,4,32]{0,3,2,1:T(8,128)S(1)}, f32[4,1,4,32]{0,3,2,1:T(8,128)S(1)}, u32[]{:S(2)}, u32[]{:S(2)}) collective-permute-start(f32[4,1,4,32]{0,3,2,1:T(8,128)S(1)} %get-tuple-element.134), channel_id=1, source_target_pairs={{0,16},{16,32},{32,48},{48,64},{64,80},{80,96},{96,112},{1,17},{17... | collective-permute-start | bytes 6152 | tf_op jit(solution)/shard_map/ppermute | solution.py:36
  290.7 21.8 %collective-permute-start.43 = (f32[4,1,4,32]{0,3,2,1:T(8,128)S(1)}, f32[4,1,4,32]{0,3,2,1:T(8,128)S(1)}, u32[]{:S(2)}, u32[]{:S(2)}) collective-permute-start(f32[4,1,4,32]{0,3,2,1:T(8,128)S(1)} %get-tuple-element.128), channel_id=1, source_target_pairs={{0,16},{16,32},{32,48},{48,64},{64,80},{80,96},{96,112},{1,17},{17... | collective-permute-start | bytes 6152 | tf_op jit(solution)/shard_map/ppermute | solution.py:36
  296.2 16.4 %collective-permute-start.42 = (f32[4,1,4,32]{0,3,2,1:T(8,128)S(1)}, f32[4,1,4,32]{0,3,2,1:T(8,128)S(1)}, u32[]{:S(2)}, u32[]{:S(2)}) collective-permute-start(f32[4,1,4,32]{0,3,2,1:T(8,128)S(1)} %get-tuple-element.129), channel_id=1, source_target_pairs={{16,0},{32,16},{48,32},{64,48},{80,64},{96,80},{112,96},{17,1},{33... | collective-permute-start | bytes 6152 | tf_op jit(solution)/shard_map/ppermute | solution.py:37
  317.5 25.1 %collective-permute-start.49 = (f32[4,1,8,64]{3,2,1,0:T(8,128)S(1)}, f32[4,1,8,64]{3,2,1,0:T(8,128)S(1)}, u32[]{:S(2)}, u32[]{:S(2)}) collective-permute-start(f32[4,1,8,64]{3,2,1,0:T(8,128)S(1)} %get-tuple-element.182), channel_id=1, source_target_pairs={{0,16},{16,32},{32,48},{48,64},{64,80},{80,96},{96,112},{1,17},{17... | collective-permute-start | bytes 24584 | tf_op jit(solution)/shard_map/ppermute | solution.py:36
  323.7 18.9 %collective-permute-start.48 = (f32[4,1,8,64]{3,2,1,0:T(8,128)S(1)}, f32[4,1,8,64]{3,2,1,0:T(8,128)S(1)}, u32[]{:S(2)}, u32[]{:S(2)}) collective-permute-start(f32[4,1,8,64]{3,2,1,0:T(8,128)S(1)} %get-tuple-element.183), channel_id=1, source_target_pairs={{16,0},{32,16},{48,32},{64,48},{80,64},{96,80},{112,96},{17,1},{33... | collective-permute-start | bytes 24584 | tf_op jit(solution)/shard_map/ppermute | solution.py:37
  325.7 17.0 %collective-permute-start.52 = (f32[4,8,1,64]{3,2,1,0:T(1,128)S(1)}, f32[4,8,1,64]{3,2,1,0:T(1,128)S(1)}, u32[]{:S(2)}, u32[]{:S(2)}) collective-permute-start(f32[4,8,1,64]{3,2,1,0:T(1,128)S(1)} %get-tuple-element.178), channel_id=1, source_target_pairs={{1,0},{2,1},{3,2},{5,4},{6,5},{7,6},{9,8},{10,9},{11,10},{13,12},{... | collective-permute-start | bytes 24584 | tf_op jit(solution)/shard_map/ppermute | solution.py:37
  327.0 15.7 %collective-permute-start.53 = (f32[4,8,1,64]{3,2,1,0:T(1,128)S(1)}, f32[4,8,1,64]{3,2,1,0:T(1,128)S(1)}, u32[]{:S(2)}, u32[]{:S(2)}) collective-permute-start(f32[4,8,1,64]{3,2,1,0:T(1,128)S(1)} %get-tuple-element.179), channel_id=1, source_target_pairs={{0,1},{1,2},{2,3},{4,5},{5,6},{6,7},{8,9},{9,10},{10,11},{12,13},{... | collective-permute-start | bytes 24584 | tf_op jit(solution)/shard_map/ppermute | solution.py:36
  343.0 25.3 %collective-permute-start.55 = (f32[4,1,8,64]{3,2,1,0:T(8,128)S(1)}, f32[4,1,8,64]{3,2,1,0:T(8,128)S(1)}, u32[]{:S(2)}, u32[]{:S(2)}) collective-permute-start(f32[4,1,8,64]{3,2,1,0:T(8,128)S(1)} %get-tuple-element.176), channel_id=1, source_target_pairs={{0,16},{16,32},{32,48},{48,64},{64,80},{80,96},{96,112},{1,17},{17... | collective-permute-start | bytes 24584 | tf_op jit(solution)/shard_map/ppermute | solution.py:36
  349.2 19.1 %collective-permute-start.54 = (f32[4,1,8,64]{3,2,1,0:T(8,128)S(1)}, f32[4,1,8,64]{3,2,1,0:T(8,128)S(1)}, u32[]{:S(2)}, u32[]{:S(2)}) collective-permute-start(f32[4,1,8,64]{3,2,1,0:T(8,128)S(1)} %get-tuple-element.177), channel_id=1, source_target_pairs={{16,0},{32,16},{48,32},{64,48},{80,64},{96,80},{112,96},{17,1},{33... | collective-permute-start | bytes 24584 | tf_op jit(solution)/shard_map/ppermute | solution.py:37
  351.2 17.1 %collective-permute-start.58 = (f32[4,8,1,64]{3,2,1,0:T(1,128)S(1)}, f32[4,8,1,64]{3,2,1,0:T(1,128)S(1)}, u32[]{:S(2)}, u32[]{:S(2)}) collective-permute-start(f32[4,8,1,64]{3,2,1,0:T(1,128)S(1)} %get-tuple-element.172), channel_id=1, source_target_pairs={{1,0},{2,1},{3,2},{5,4},{6,5},{7,6},{9,8},{10,9},{11,10},{13,12},{... | collective-permute-start | bytes 24584 | tf_op jit(solution)/shard_map/ppermute | solution.py:37
  352.5 15.9 %collective-permute-start.59 = (f32[4,8,1,64]{3,2,1,0:T(1,128)S(1)}, f32[4,8,1,64]{3,2,1,0:T(1,128)S(1)}, u32[]{:S(2)}, u32[]{:S(2)}) collective-permute-start(f32[4,8,1,64]{3,2,1,0:T(1,128)S(1)} %get-tuple-element.173), channel_id=1, source_target_pairs={{0,1},{1,2},{2,3},{4,5},{5,6},{6,7},{8,9},{9,10},{10,11},{12,13},{... | collective-permute-start | bytes 24584 | tf_op jit(solution)/shard_map/ppermute | solution.py:36
  588.5 24.7 %collective-permute-start.91 = (f32[4,1,8,64]{3,2,1,0:T(8,128)S(1)}, f32[4,1,8,64]{3,2,1,0:T(8,128)S(1)}, u32[]{:S(2)}, u32[]{:S(2)}) collective-permute-start(f32[4,1,8,64]{3,2,1,0:T(8,128)S(1)} %get-tuple-element.170), channel_id=1, source_target_pairs={{0,16},{16,32},{32,48},{48,64},{64,80},{80,96},{96,112},{1,17},{17... | collective-permute-start | bytes 24584 | tf_op jit(solution)/shard_map/ppermute | solution.py:36
  592.6 20.7 %collective-permute-start.90 = (f32[4,1,8,64]{3,2,1,0:T(8,128)S(1)}, f32[4,1,8,64]{3,2,1,0:T(8,128)S(1)}, u32[]{:S(2)}, u32[]{:S(2)}) collective-permute-start(f32[4,1,8,64]{3,2,1,0:T(8,128)S(1)} %get-tuple-element.171), channel_id=1, source_target_pairs={{16,0},{32,16},{48,32},{64,48},{80,64},{96,80},{112,96},{17,1},{33... | collective-permute-start | bytes 24584 | tf_op jit(solution)/shard_map/ppermute | solution.py:37
  594.5 18.7 %collective-permute-start.94 = (f32[4,8,1,64]{3,2,1,0:T(1,128)S(1)}, f32[4,8,1,64]{3,2,1,0:T(1,128)S(1)}, u32[]{:S(2)}, u32[]{:S(2)}) collective-permute-start(f32[4,8,1,64]{3,2,1,0:T(1,128)S(1)} %get-tuple-element.166), channel_id=1, source_target_pairs={{1,0},{2,1},{3,2},{5,4},{6,5},{7,6},{9,8},{10,9},{11,10},{13,12},{... | collective-permute-start | bytes 24584 | tf_op jit(solution)/shard_map/ppermute | solution.py:37
  595.8 17.4 %collective-permute-start.95 = (f32[4,8,1,64]{3,2,1,0:T(1,128)S(1)}, f32[4,8,1,64]{3,2,1,0:T(1,128)S(1)}, u32[]{:S(2)}, u32[]{:S(2)}) collective-permute-start(f32[4,8,1,64]{3,2,1,0:T(1,128)S(1)} %get-tuple-element.167), channel_id=1, source_target_pairs={{0,1},{1,2},{2,3},{4,5},{5,6},{6,7},{8,9},{9,10},{10,11},{12,13},{... | collective-permute-start | bytes 24584 | tf_op jit(solution)/shard_map/ppermute | solution.py:36
  613.6 24.3 %collective-permute-start.97 = (f32[4,1,8,64]{3,2,1,0:T(8,128)S(1)}, f32[4,1,8,64]{3,2,1,0:T(8,128)S(1)}, u32[]{:S(2)}, u32[]{:S(2)}) collective-permute-start(f32[4,1,8,64]{3,2,1,0:T(8,128)S(1)} %get-tuple-element.164), channel_id=1, source_target_pairs={{0,16},{16,32},{32,48},{48,64},{64,80},{80,96},{96,112},{1,17},{17... | collective-permute-start | bytes 24584 | tf_op jit(solution)/shard_map/ppermute | solution.py:36
  618.3 19.6 %collective-permute-start.96 = (f32[4,1,8,64]{3,2,1,0:T(8,128)S(1)}, f32[4,1,8,64]{3,2,1,0:T(8,128)S(1)}, u32[]{:S(2)}, u32[]{:S(2)}) collective-permute-start(f32[4,1,8,64]{3,2,1,0:T(8,128)S(1)} %get-tuple-element.165), channel_id=1, source_target_pairs={{16,0},{32,16},{48,32},{64,48},{80,64},{96,80},{112,96},{17,1},{33... | collective-permute-start | bytes 24584 | tf_op jit(solution)/shard_map/ppermute | solution.py:37
  620.2 17.7 %collective-permute-start.100 = (f32[4,8,1,64]{3,2,1,0:T(1,128)S(1)}, f32[4,8,1,64]{3,2,1,0:T(1,128)S(1)}, u32[]{:S(2)}, u32[]{:S(2)}) collective-permute-start(f32[4,8,1,64]{3,2,1,0:T(1,128)S(1)} %get-tuple-element.160), channel_id=1, source_target_pairs={{1,0},{2,1},{3,2},{5,4},{6,5},{7,6},{9,8},{10,9},{11,10},{13,12},{... | collective-permute-start | bytes 24584 | tf_op jit(solution)/shard_map/ppermute | solution.py:37
  621.5 16.4 %collective-permute-start.101 = (f32[4,8,1,64]{3,2,1,0:T(1,128)S(1)}, f32[4,8,1,64]{3,2,1,0:T(1,128)S(1)}, u32[]{:S(2)}, u32[]{:S(2)}) collective-permute-start(f32[4,8,1,64]{3,2,1,0:T(1,128)S(1)} %get-tuple-element.161), channel_id=1, source_target_pairs={{0,1},{1,2},{2,3},{4,5},{5,6},{6,7},{8,9},{9,10},{10,11},{12,13},{... | collective-permute-start | bytes 24584 | tf_op jit(solution)/shard_map/ppermute | solution.py:36
  643.5 22.1 %collective-permute-start.103 = (f32[4,1,4,32]{0,3,2,1:T(8,128)S(1)}, f32[4,1,4,32]{0,3,2,1:T(8,128)S(1)}, u32[]{:S(2)}, u32[]{:S(2)}) collective-permute-start(f32[4,1,4,32]{0,3,2,1:T(8,128)S(1)} %get-tuple-element.122), channel_id=1, source_target_pairs={{0,16},{16,32},{32,48},{48,64},{64,80},{80,96},{96,112},{1,17},{17... | collective-permute-start | bytes 6152 | tf_op jit(solution)/shard_map/ppermute | solution.py:36
  649.1 16.5 %collective-permute-start.102 = (f32[4,1,4,32]{0,3,2,1:T(8,128)S(1)}, f32[4,1,4,32]{0,3,2,1:T(8,128)S(1)}, u32[]{:S(2)}, u32[]{:S(2)}) collective-permute-start(f32[4,1,4,32]{0,3,2,1:T(8,128)S(1)} %get-tuple-element.123), channel_id=1, source_target_pairs={{16,0},{32,16},{48,32},{64,48},{80,64},{96,80},{112,96},{17,1},{33... | collective-permute-start | bytes 6152 | tf_op jit(solution)/shard_map/ppermute | solution.py:37
  665.9 22.7 %collective-permute-start.109 = (f32[4,1,4,32]{0,3,2,1:T(8,128)S(1)}, f32[4,1,4,32]{0,3,2,1:T(8,128)S(1)}, u32[]{:S(2)}, u32[]{:S(2)}) collective-permute-start(f32[4,1,4,32]{0,3,2,1:T(8,128)S(1)} %get-tuple-element.116), channel_id=1, source_target_pairs={{0,16},{16,32},{32,48},{48,64},{64,80},{80,96},{96,112},{1,17},{17... | collective-permute-start | bytes 6152 | tf_op jit(solution)/shard_map/ppermute | solution.py:36
  672.1 16.5 %collective-permute-start.108 = (f32[4,1,4,32]{0,3,2,1:T(8,128)S(1)}, f32[4,1,4,32]{0,3,2,1:T(8,128)S(1)}, u32[]{:S(2)}, u32[]{:S(2)}) collective-permute-start(f32[4,1,4,32]{0,3,2,1:T(8,128)S(1)} %get-tuple-element.117), channel_id=1, source_target_pairs={{16,0},{32,16},{48,32},{64,48},{80,64},{96,80},{112,96},{17,1},{33... | collective-permute-start | bytes 6152 | tf_op jit(solution)/shard_map/ppermute | solution.py:37
  724.0 17.5 %collective-permute-start.115 = (f32[4,1,4,32]{0,3,2,1:T(8,128)S(1)}, f32[4,1,4,32]{0,3,2,1:T(8,128)S(1)}, u32[]{:S(2)}, u32[]{:S(2)}) collective-permute-start(f32[4,1,4,32]{0,3,2,1:T(8,128)S(1)} %get-tuple-element.110), channel_id=1, source_target_pairs={{0,16},{16,32},{32,48},{48,64},{64,80},{80,96},{96,112},{1,17},{17... | collective-permute-start | bytes 6152 | tf_op jit(solution)/shard_map/ppermute | solution.py:36
  726.6 14.9 %collective-permute-start.114 = (f32[4,1,4,32]{0,3,2,1:T(8,128)S(1)}, f32[4,1,4,32]{0,3,2,1:T(8,128)S(1)}, u32[]{:S(2)}, u32[]{:S(2)}) collective-permute-start(f32[4,1,4,32]{0,3,2,1:T(8,128)S(1)} %get-tuple-element.111), channel_id=1, source_target_pairs={{16,0},{32,16},{48,32},{64,48},{80,64},{96,80},{112,96},{17,1},{33... | collective-permute-start | bytes 6152 | tf_op jit(solution)/shard_map/ppermute | solution.py:37
  741.8 22.6 %collective-permute-start.121 = (f32[4,1,4,32]{0,3,2,1:T(8,128)S(1)}, f32[4,1,4,32]{0,3,2,1:T(8,128)S(1)}, u32[]{:S(2)}, u32[]{:S(2)}) collective-permute-start(f32[4,1,4,32]{0,3,2,1:T(8,128)S(1)} %get-tuple-element.104), channel_id=1, source_target_pairs={{0,16},{16,32},{32,48},{48,64},{64,80},{80,96},{96,112},{1,17},{17... | collective-permute-start | bytes 6152 | tf_op jit(solution)/shard_map/ppermute | solution.py:36
  748.0 16.4 %collective-permute-start.120 = (f32[4,1,4,32]{0,3,2,1:T(8,128)S(1)}, f32[4,1,4,32]{0,3,2,1:T(8,128)S(1)}, u32[]{:S(2)}, u32[]{:S(2)}) collective-permute-start(f32[4,1,4,32]{0,3,2,1:T(8,128)S(1)} %get-tuple-element.105), channel_id=1, source_target_pairs={{16,0},{32,16},{48,32},{64,48},{80,64},{96,80},{112,96},{17,1},{33... | collective-permute-start | bytes 6152 | tf_op jit(solution)/shard_map/ppermute | solution.py:37
  769.4 25.1 %collective-permute-start.127 = (f32[4,1,8,64]{3,2,1,0:T(8,128)S(1)}, f32[4,1,8,64]{3,2,1,0:T(8,128)S(1)}, u32[]{:S(2)}, u32[]{:S(2)}) collective-permute-start(f32[4,1,8,64]{3,2,1,0:T(8,128)S(1)} %get-tuple-element.158), channel_id=1, source_target_pairs={{0,16},{16,32},{32,48},{48,64},{64,80},{80,96},{96,112},{1,17},{17... | collective-permute-start | bytes 24584 | tf_op jit(solution)/shard_map/ppermute | solution.py:36
  775.6 18.9 %collective-permute-start.126 = (f32[4,1,8,64]{3,2,1,0:T(8,128)S(1)}, f32[4,1,8,64]{3,2,1,0:T(8,128)S(1)}, u32[]{:S(2)}, u32[]{:S(2)}) collective-permute-start(f32[4,1,8,64]{3,2,1,0:T(8,128)S(1)} %get-tuple-element.159), channel_id=1, source_target_pairs={{16,0},{32,16},{48,32},{64,48},{80,64},{96,80},{112,96},{17,1},{33... | collective-permute-start | bytes 24584 | tf_op jit(solution)/shard_map/ppermute | solution.py:37
  777.5 17.0 %collective-permute-start.130 = (f32[4,8,1,64]{3,2,1,0:T(1,128)S(1)}, f32[4,8,1,64]{3,2,1,0:T(1,128)S(1)}, u32[]{:S(2)}, u32[]{:S(2)}) collective-permute-start(f32[4,8,1,64]{3,2,1,0:T(1,128)S(1)} %get-tuple-element.154), channel_id=1, source_target_pairs={{1,0},{2,1},{3,2},{5,4},{6,5},{7,6},{9,8},{10,9},{11,10},{13,12},{... | collective-permute-start | bytes 24584 | tf_op jit(solution)/shard_map/ppermute | solution.py:37
  778.8 15.7 %collective-permute-start.131 = (f32[4,8,1,64]{3,2,1,0:T(1,128)S(1)}, f32[4,8,1,64]{3,2,1,0:T(1,128)S(1)}, u32[]{:S(2)}, u32[]{:S(2)}) collective-permute-start(f32[4,8,1,64]{3,2,1,0:T(1,128)S(1)} %get-tuple-element.155), channel_id=1, source_target_pairs={{0,1},{1,2},{2,3},{4,5},{5,6},{6,7},{8,9},{9,10},{10,11},{12,13},{... | collective-permute-start | bytes 24584 | tf_op jit(solution)/shard_map/ppermute | solution.py:36
  794.9 25.3 %collective-permute-start.133 = (f32[4,1,8,64]{3,2,1,0:T(8,128)S(1)}, f32[4,1,8,64]{3,2,1,0:T(8,128)S(1)}, u32[]{:S(2)}, u32[]{:S(2)}) collective-permute-start(f32[4,1,8,64]{3,2,1,0:T(8,128)S(1)} %get-tuple-element.152), channel_id=1, source_target_pairs={{0,16},{16,32},{32,48},{48,64},{64,80},{80,96},{96,112},{1,17},{17... | collective-permute-start | bytes 24584 | tf_op jit(solution)/shard_map/ppermute | solution.py:36
  801.1 19.1 %collective-permute-start.132 = (f32[4,1,8,64]{3,2,1,0:T(8,128)S(1)}, f32[4,1,8,64]{3,2,1,0:T(8,128)S(1)}, u32[]{:S(2)}, u32[]{:S(2)}) collective-permute-start(f32[4,1,8,64]{3,2,1,0:T(8,128)S(1)} %get-tuple-element.153), channel_id=1, source_target_pairs={{16,0},{32,16},{48,32},{64,48},{80,64},{96,80},{112,96},{17,1},{33... | collective-permute-start | bytes 24584 | tf_op jit(solution)/shard_map/ppermute | solution.py:37
  803.0 17.1 %collective-permute-start.136 = (f32[4,8,1,64]{3,2,1,0:T(1,128)S(1)}, f32[4,8,1,64]{3,2,1,0:T(1,128)S(1)}, u32[]{:S(2)}, u32[]{:S(2)}) collective-permute-start(f32[4,8,1,64]{3,2,1,0:T(1,128)S(1)} %get-tuple-element.148), channel_id=1, source_target_pairs={{1,0},{2,1},{3,2},{5,4},{6,5},{7,6},{9,8},{10,9},{11,10},{13,12},{... | collective-permute-start | bytes 24584 | tf_op jit(solution)/shard_map/ppermute | solution.py:37
  804.3 15.9 %collective-permute-start.137 = (f32[4,8,1,64]{3,2,1,0:T(1,128)S(1)}, f32[4,8,1,64]{3,2,1,0:T(1,128)S(1)}, u32[]{:S(2)}, u32[]{:S(2)}) collective-permute-start(f32[4,8,1,64]{3,2,1,0:T(1,128)S(1)} %get-tuple-element.149), channel_id=1, source_target_pairs={{0,1},{1,2},{2,3},{4,5},{5,6},{6,7},{8,9},{9,10},{10,11},{12,13},{... | collective-permute-start | bytes 24584 | tf_op jit(solution)/shard_map/ppermute | solution.py:36
  (119 other events, 965.0 us)
